TPU v7x, 32 devices: a whole 2x2x4 slice. The times are simulated.
32 devices in a mesh: grp: 8 (over z, x), brick: 4 (over y, core).
Axes of the slice: x: 2, y: 2, z: 4, core: 2. Of those that a mesh axis runs over, the one named last changes fastest.
Arguments:
- deformation_vector: float32 [3, 32, 64, 256], P(None, 'grp', 'brick'), may hold values from -4 to 4
- applied_traction: float32 [3, 32, 64, 256], P(None, 'grp', 'brick'), may hold values from 4 to 16
- heat_level: float32 [32, 64, 256], P('grp', 'brick'), may hold values from -6 to 6
- stiffness_main_terms: float32 [3, 32, 64, 256], P(None, 'grp', 'brick'), may hold values from 8 to 10
- stiffness_cross_terms: float32 [3, 32, 64, 256], P(None, 'grp', 'brick'), may hold values from -0.8 to 0.8
- normal_clearance: float32 [32, 64, 256], P('grp', 'brick'), may hold values from -0.5 to 1
- touching_flag: int32 [32, 64, 256], P('grp', 'brick'), may hold values 0 or 1
- clipped_normal_flag: int32 [32, 64, 256], P('grp', 'brick'), may hold values 0 or 1
Outputs:
- moved: float32 [3, 32, 64, 256], P(None, 'grp', 'brick')
- residual: float32 [3, 32, 64, 256], P(None, 'grp', 'brick')
All inputs are finite; a program needn't handle non-finite values. No bound on the sum of `touching_flag` or of `clipped_normal_flag` on one device may be relied on, other than what follows from the above.
Results may differ from a plain program's by a relative error of at most 0.00002.
Values sent between devices are 32-bit elements; how exact they have to be, the bound alone decides.
A program may use at most 128 MiB of HBM per device.

v0:
```python
import jax
import jax.numpy as jnp
from jax import lax
from jax.experimental import pallas as pl
from jax.experimental.pallas import tpu as pltpu
from jax.sharding import PartitionSpec as P

OMEGA = 0.6
FREE = 1000.0
EXCHANGES = 11
FINE = (0, 1, 2, 8, 9, 10)
DEPTH = {3: 3, 4: 2, 5: 1, 6: 2}
USED = FINE + tuple(DEPTH)
TWICE = (3, 6)
MESH = pl.DeviceIdType.MESH


def inverse(k):
    a, b, c, d, e, f = k
    i00 = b * c - e * e
    i11 = a * c - f * f
    i22 = a * b - d * d
    i01 = f * e - d * c
    i12 = d * f - a * e
    i02 = d * e - b * f
    scale = 1.0 / (a * i00 + d * i01 + f * i02)
    return [i00 * scale, i11 * scale, i22 * scale, i01 * scale, i12 * scale, i02 * scale]


def symmetric_times(m, v):
    return [
        m[0] * v[0] + m[3] * v[1] + m[5] * v[2],
        m[3] * v[0] + m[1] * v[1] + m[4] * v[2],
        m[5] * v[0] + m[4] * v[1] + m[2] * v[2],
    ]


def kernel(
    disp_h, load_h, heat_h, diag_h, off_h, clear_h, touch_h, clip_h,
    moved, resid,
    first, fine, middle, xs, xr, ys, yr, ds, dr, halo_x, halo_y, load, stiff, clear, touch, clip,
    force, inv1, obst1, g2, k2, inv2, obst2, g3, k3, inv3, obst3,
    in_sem, send_sem, recv_sem, dsend_sem, drecv_sem,
):
    X, Y, Z = heat_h.shape
    X2, X3 = X // 2, X // 4
    g, b = lax.axis_index("grp"), lax.axis_index("brick")
    ng, nb = lax.axis_size("grp"), lax.axis_size("brick")
    ways = (
        ("grp", g - 1, g > 0),
        ("grp", g + 1, g < ng - 1),
        ("brick", b - 1, b > 0),
        ("brick", b + 1, b < nb - 1),
    )
    barrier = pltpu.get_barrier_semaphore()
    for axis, there, has in ways:

        @pl.when(has)
        def _():
            pl.semaphore_signal(barrier, inc=1, device_id={axis: there}, device_id_type=MESH)

    corners = [
        (ways[p][1], ways[2 + q][1], ways[p][2] & ways[2 + q][2]) for p in (0, 1) for q in (0, 1)
    ]
    for at, beyond, has in corners:

        @pl.when(has)
        def _():
            pl.semaphore_signal(
                barrier, inc=1, device_id={"grp": at, "brick": beyond}, device_id_type=MESH
            )

    pairs = (
        (disp_h, first.at[0:3, 1 : X + 1]),
        (heat_h, first.at[3, 1 : X + 1]),
        (diag_h, stiff.at[0:3]),
        (off_h, stiff.at[3:6]),
        (load_h, load),
        (clear_h, clear),
        (touch_h, touch),
        (clip_h, clip),
    )
    arriving = [pltpu.make_async_copy(s, d, in_sem.at[i]) for i, (s, d) in enumerate(pairs)]
    for copy in arriving:
        copy.start()

    row = lax.broadcasted_iota(jnp.int32, (Y, Z), 0)
    lane = lax.broadcasted_iota(jnp.int32, (Y, Z), 1)
    lanes = {8: lax.broadcasted_iota(jnp.int32, (8, Z), 1), Y: lane}
    even_row = (row & 1) == 0
    even_lane = (lane & 1) == 0

    def fine_ref(k):
        return first if k == 0 else fine.at[FINE.index(k) - 1]

    for way, (axis, there, has) in enumerate(ways):

        @pl.when(jnp.logical_not(has))
        def _():
            for k in USED:
                if way >= 2:
                    yr[k, way - 2] = jnp.zeros(yr.shape[2:], jnp.float32)
                elif k in FINE:
                    for c in range(4 if k == 0 else 3):
                        fine_ref(k)[c, 0 if way == 0 else X + 1] = jnp.zeros((Y, Z), jnp.float32)
                else:
                    for n in range(DEPTH[k]):
                        xr[k, way, n] = jnp.zeros((Y, Z), jnp.float32)

    for n, (_, _, has) in enumerate(corners):

        @pl.when(jnp.logical_not(has))
        def _():
            for k in range(2):
                dr[k, n] = jnp.zeros((8, Z), jnp.float32)

    def rows_of(k):
        count = 4 * X if k == 0 else 3 * X if k in FINE else {3: 10, 4: 6, 5: 3, 6: 6}[k] * X2
        return -(-count // 8) * 8

    def transfer(k, way):
        if way >= 2:
            n = way - 2
            src, dst = ys.at[k, n, 0 : rows_of(k)], yr.at[k, 1 - n, 0 : rows_of(k)]
        elif k in FINE:
            ref = fine_ref(k)
            src, dst = ref.at[:, X if way else 1], ref.at[:, 0 if way else X + 1]
        else:
            src, dst = xs.at[k, way, 0 : DEPTH[k]], xr.at[k, 1 - way, 0 : DEPTH[k]]
        axis, there, _ = ways[way]
        return pltpu.make_async_remote_copy(
            src_ref=src,
            dst_ref=dst,
            send_sem=send_sem.at[k, way],
            recv_sem=recv_sem.at[k, way ^ 1],
            device_id={axis: there},
            device_id_type=MESH,
        )

    def begin(k, sides=(0, 1, 2, 3)):
        for way in sides:

            @pl.when(ways[way][2])
            def _():
                transfer(k, way).start()

    def arrive(k, sides):
        for side in sides:

            @pl.when(ways[side][2])
            def _():
                transfer(k, side ^ 1).wait_recv()

    def leave(k):
        for way in range(4):

            @pl.when(ways[way][2])
            def _():
                transfer(k, way).wait_send()

    def cross(k, n):
        at, beyond, _ = corners[n]
        return pltpu.make_async_remote_copy(
            src_ref=ds.at[TWICE.index(k), n],
            dst_ref=dr.at[TWICE.index(k), 3 - n],
            send_sem=dsend_sem.at[TWICE.index(k), n],
            recv_sem=drecv_sem.at[TWICE.index(k), 3 - n],
            device_id={"grp": at, "brick": beyond},
            device_id_type=MESH,
        )

    def cross_all(k, what):
        for n in range(4):

            @pl.when(corners[3 - n if what == "arrive" else n][2])
            def _():
                copy = cross(k, n)
                if what == "begin":
                    copy.start()
                elif what == "arrive":
                    copy.wait_recv()
                else:
                    copy.wait_send()

    def edge_rows(k, layers, c, i, v):
        n = c * layers + i
        ys[k, 0, n : n + 1, :] = v[0:1, :]
        ys[k, 1, n : n + 1, :] = v[Y - 1 : Y, :]

    def before(v, s):
        return jnp.where(lanes[v.shape[0]] < s, 0.0, pltpu.roll(v, s, 1))

    def after(v, s):
        return jnp.where(lanes[v.shape[0]] >= Z - s, 0.0, pltpu.roll(v, Z - s, 1))

    def above(k, layers, c, i, v, s):
        n = c * layers + i
        return jnp.where(row < s, yr[k, 0, n : n + 1, :], pltpu.roll(v, s, 0))

    def below(k, layers, c, i, v, s):
        n = c * layers + i
        return jnp.where(row >= Y - s, yr[k, 1, n : n + 1, :], pltpu.roll(v, Y - s, 0))

    def pair_lane(v, s, how):
        return how(v, jnp.where((lane & s) == 0, pltpu.roll(v, Z - s, 1), pltpu.roll(v, s, 1)))

    def pair_row(v, s, how):
        return how(v, jnp.where((row & s) == 0, pltpu.roll(v, Y - s, 0), pltpu.roll(v, s, 0)))

    def group(v, w, s, how):
        return pair_row(pair_lane(how(v, w), s, how), s, how)

    def plus(v, w):
        return v + w

    def pack(v):
        odd = v[2] if len(v) == 3 else jnp.where(even_row, v[2], v[3])
        return jnp.where(even_lane, jnp.where(even_row, v[0], v[1]), odd)

    def split(q):
        return [
            jnp.where(even_row, q, pltpu.roll(q, 1, 0)),
            jnp.where(even_row, pltpu.roll(q, Y - 1, 0), q),
        ]

    def unpack(p, four=False):
        odd = jnp.where(even_lane, pltpu.roll(p, Z - 1, 1), p)
        return split(jnp.where(even_lane, p, pltpu.roll(p, 1, 1))) + (split(odd) if four else [odd])

    def layer(ref, i, count=3):
        return [ref[c, i] for c in range(count)]

    def put(ref, i, values):
        for c, v in enumerate(values):
            ref[c, i] = v

    def stage(k, layers, s, value, blocks, right, halo, finish):
        if k > 0:
            arrive(k, (2, 3))

        def partial(i):
            v = value(i)
            kv = symmetric_times(blocks(i), v)
            g = right(i)
            rest = []
            for c in range(3):
                near = above(k, layers, c, i, v[c], s) + below(k, layers, c, i, v[c], s)
                near = near + (before(v[c], s) + after(v[c], s))
                rest.append((g[c] - kv[c]) + near)
            for n in (i - 1, i + 1):
                if 0 <= n < layers:
                    rest = [r + x for r, x in zip(rest, value(n))]
            return rest

        for i in range(1, layers - 1):
            finish(i, value(i), partial(i))
        ends = {i: partial(i) for i in {0, layers - 1}}
        for side, i in ((0, 0), (1, layers - 1)):
            arrive(k, (side,))
            ends[i] = [r + x for r, x in zip(ends[i], halo(side))]
            if side == 1 or layers > 1:
                finish(i, value(i), ends[i])

    def relaxed(v, inv, rest, obstacle):
        step = symmetric_times(inv, rest)
        w = [v[c] + OMEGA * step[c] for c in range(3)]
        return [jnp.minimum(w[0], obstacle), w[1], w[2]]

    def opened(inv, right, obstacle):
        w = [OMEGA * x for x in symmetric_times(inv, right)]
        return [jnp.minimum(w[0], obstacle), w[1], w[2]]

    def fine_stage(k, finish, halo=None):
        ref = fine_ref(k)
        stage(
            k,
            X,
            1,
            lambda i: layer(ref, i + 1),
            lambda i: layer(stiff, i, 6),
            lambda i: layer(force, i),
            halo or (lambda side: layer(ref, (X + 1) * side)),
            finish,
        )

    def fine_store(to, i, w):
        put(fine_ref(to), i + 1, w)
        for side, end in ((0, 0), (1, X - 1)):
            if i == end:
                begin(to, (side,))
        for c in range(3):
            edge_rows(to, X, c, i, w[c])

    def fine_sweep(k, to, halo=None):
        def finish(i, v, rest):
            w = relaxed(v, layer(inv1, i, 6), rest, obst1[i])
            fine_store(to, i, w)
            if to == 10:
                put(moved, i, w)

        fine_stage(k, finish, halo)
        begin(to, (2, 3))

    arriving[0].wait()
    arriving[1].wait()
    pl.semaphore_wait(barrier, sum(jnp.where(has, 1, 0) for _, _, has in ways + tuple(corners)))
    begin(0, (0, 1))
    for c in range(4):
        for i in range(X):
            edge_rows(0, X, c, i, first[c, i + 1])
    begin(0, (2, 3))
    for copy in arriving[2:]:
        copy.wait()
    for i in range(X):
        put(inv1, i, inverse(layer(stiff, i, 6)))
        obst1[i] = jnp.where(touch[i] == 1, clear[i], FREE)
    arrive(0, (2, 3))
    for i in range(X):
        h = first[3, i + 1]
        along = load[0, i]
        if i > 0:
            along = along + first[3, i]
        if i < X - 1:
            along = along - first[3, i + 2]
        force[0, i] = along
        force[1, i] = load[1, i] - (below(0, X, 3, i, h, 1) - above(0, X, 3, i, h, 1))
        force[2, i] = load[2, i] - (after(h, 1) - before(h, 1))

    def first_halo(side):
        v = layer(first, (X + 1) * side)
        heat = first[3, (X + 1) * side]
        heat = heat if side == 0 else -heat
        end = (X - 1) * side
        force[0, end] = force[0, end] + heat
        return [v[0] + heat, v[1], v[2]]

    fine_sweep(0, 1, first_halo)
    for j in range(X2):
        k = [0.125 * group(stiff[c, 2 * j], stiff[c, 2 * j + 1], 1, plus) for c in range(6)]
        put(k2, j, k)
        put(inv2, j, inverse(k))
        for side, end in ((0, 0), (1, X2 - 1)):
            if j == end:
                xs[4, side, 0] = pack(k[0:4])
                xs[4, side, 1] = pack([k[4], k[5], k[5]])
        for c in range(6):
            edge_rows(4, X2, c, j, k[c])
    begin(4)
    fine_sweep(1, 2)
    arrive(4, (0, 1, 2, 3))
    for side in (0, 1):
        k = unpack(xr[4, side, 0], True) + unpack(xr[4, side, 1])[0:2]
        for c, x in enumerate(k + inverse(k)):
            halo_x[side, c] = x
        for j in range(X2):
            k = [
                jnp.broadcast_to(yr[4, side, c * X2 + j : c * X2 + j + 1, :], (8, Z))
                for c in range(6)
            ]
            for c, x in enumerate(k + inverse(k)):
                halo_y[side, j, c] = x
    for j in range(X3):
        k = [0.125 * group(k2[c, 2 * j], k2[c, 2 * j + 1], 2, plus) for c in range(6)]
        put(k3, j, k)
        put(inv3, j, inverse(k))
    for j in range(X2):
        gaps = []
        for i in (2 * j, 2 * j + 1):
            allowed = (touch[i] == 1) & (clip[i] == 0)
            gaps.append(jnp.where(allowed, clear[i] - fine_ref(2)[0, i + 1], FREE))
        obst2[j] = group(gaps[0], gaps[1], 1, jnp.minimum)

    def coarse_store(k, layers, m, j, v):
        for side, end in ((0, 0), (1, layers - 1)):
            if j == end:
                xs[k, side, 0] = pack(v)
        put(m, j, v)
        for c in range(3):
            edge_rows(k, layers, c, j, v[c])
        for side, end in ((0, 0), (1, layers - 1)):
            if j == end:
                begin(k, (side,))

    def coarse_stage(k, layers, s, m, blocks, right, finish):
        stage(
            k,
            layers,
            s,
            lambda j: layer(m, j),
            lambda j: layer(blocks, j, 6),
            lambda j: layer(right, j),
            lambda side: unpack(xr[k, side, 0]),
            finish,
        )

    def twice_begin(k, m):
        for side, near, far in ((0, 0, 1), (1, X2 - 1, X2 - 2)):
            xs[k, side, 0] = pack(layer(m, near))
            xs[k, side, 1] = pack(layer(m, far))
            if k == 3:
                xs[k, side, 2] = pack(layer(g2, near) + [obst2[near]])
            begin(k, (side,))
        for p, end in ((0, 0), (1, X2 - 1)):
            for q, at in ((0, 0), (1, Y - 1)):
                for c in range(3):
                    ds[TWICE.index(k), 2 * p + q, c : c + 1, :] = m[c, end, at : at + 1, :]
        cross_all(k, "begin")
        for j in range(X2):
            v = layer(m, j)
            rows = v + [None] * 3
            if k == 3:
                rows = rows + layer(g2, j) + [obst2[j]]
            for n, x in enumerate(rows):
                if x is not None:
                    edge_rows(k, X2, n, j, x)
            for c in range(3):
                n = (3 + c) * X2 + j
                ys[k, 0, n : n + 1, :] = v[c][2:3, :]
                ys[k, 1, n : n + 1, :] = v[c][Y - 3 : Y - 2, :]
        begin(k, (2, 3))

    def twice(k, m, keep, finish):
        def spill(side, n, j):
            return yr[k, side, n * X2 + j : n * X2 + j + 1, :]

        def wide(x):
            return jnp.broadcast_to(x, (8, Z))

        def rest_at(v, low, high, top, bottom, blocks, right):
            kv = symmetric_times(blocks, v)
            rest = []
            for c in range(3):
                if v[c].shape[0] == 8:
                    rise, fall = top[c], bottom[c]
                else:
                    rise = jnp.where(row < 2, top[c], pltpu.roll(v[c], 2, 0))
                    fall = jnp.where(row >= Y - 2, bottom[c], pltpu.roll(v[c], Y - 2, 0))
                near = (low[c] + high[c]) + (rise + fall) + (before(v[c], 2) + after(v[c], 2))
                rest.append(right[c] - kv[c] + near)
            return rest

        own = [layer(m, j) for j in range(X2)]
        arrive(k, (2, 3))
        arrive(k, (0, 1))
        cross_all(k, "arrive")
        xh = [[unpack(xr[k, side, n]) for n in (0, 1)] for side in (0, 1)]
        ext = [xh[0][0]] + own + [xh[1][0]]
        done = [None] * (X2 + 2)
        for j in range(X2):
            top, bottom = ([spill(side, c, j) for c in range(3)] for side in (0, 1))
            rest = rest_at(own[j], ext[j], ext[j + 2], top, bottom, layer(k2, j, 6), layer(g2, j))
            done[j + 1] = relaxed(own[j], layer(inv2, j, 6), rest, obst2[j])
            put(keep, j, done[j + 1])

        def corner(p, q):
            return [dr[TWICE.index(k), 2 * p + q, c : c + 1, :] for c in range(3)]

        for side in (0, 1):
            if k == 3:
                for c, x in enumerate(unpack(xr[3, side, 2], True)):
                    halo_x[side, 12 + c] = x
            st = [halo_x[side, c] for c in range(16)]
            inner = own[0] if side == 0 else own[X2 - 1]
            v = xh[side][0]
            rest = rest_at(v, xh[side][1], inner, corner(side, 0), corner(side, 1), st, st[12:15])
            w = relaxed(v, st[6:12], rest, st[15])
            done[(X2 + 1) * side] = [jnp.where(ways[side][2], x, 0.0) for x in w]
        rims = []
        for side in (0, 1):
            line = [[wide(spill(side, c, j)) for c in range(3)] for j in range(X2)]
            line = [[wide(x) for x in corner(0, side)]] + line
            line = line + [[wide(x) for x in corner(1, side)]]
            rims.append([])
            for j in range(X2):
                st = [halo_y[side, j, c] for c in range(12)]
                st = st + [wide(yr[3, side, n * X2 + j : n * X2 + j + 1, :]) for n in range(6, 10)]
                far = [wide(spill(side, 3 + c, j)) for c in range(3)]
                at = 0 if side == 0 else Y - 1
                inner = [wide(m[c, j, at : at + 1, :]) for c in range(3)]
                v = line[j + 1]
                rest = rest_at(v, line[j], line[j + 2], far, inner, st, st[12:15])
                w = relaxed(v, st[6:12], rest, st[15])
                rims[side].append([jnp.where(ways[2 + side][2], x, 0.0)[0:1, :] for x in w])
        for j in range(X2):
            rest = rest_at(
                done[j + 1], done[j], done[j + 2], rims[0][j], rims[1][j],
                layer(k2, j, 6), layer(g2, j),
            )
            finish(j, done[j + 1], rest)

    m0, m1, m2, m3, m4 = (middle.at[n] for n in range(5))
    fine_rests = {}

    def restrict(i, v, rest):
        fine_rests[i] = [jnp.where(clip[i] == 1, 0.0, rest[0]), rest[1], rest[2]]
        j = i // 2
        if 2 * j in fine_rests and 2 * j + 1 in fine_rests:
            pair = fine_rests[2 * j], fine_rests[2 * j + 1]
            right = [0.25 * group(pair[0][c], pair[1][c], 1, plus) for c in range(3)]
            put(g2, j, right)
            put(m0, j, opened(layer(inv2, j, 6), right, obst2[j]))

    fine_stage(2, restrict)
    twice_begin(3, m0)

    middle_rests = {}

    def restrict_again(i, v, rest):
        middle_rests[i] = rest
        j = i // 2
        if 2 * j in middle_rests and 2 * j + 1 in middle_rests:
            pair = middle_rests[2 * j], middle_rests[2 * j + 1]
            right = [0.25 * group(pair[0][c], pair[1][c], 2, plus) for c in range(3)]
            gaps = [obst2[n] - m1[0, n] for n in (2 * j, 2 * j + 1)]
            obst3[j] = group(gaps[0], gaps[1], 2, jnp.minimum)
            put(g3, j, right)
            coarse_store(5, X3, m4, j, opened(layer(inv3, j, 6), right, obst3[j]))

    twice(3, m0, m1, restrict_again)
    begin(5, (2, 3))

    def lowest(j, v, rest):
        low = relaxed(v, layer(inv3, j, 6), rest, obst3[j])
        for n in (2 * j, 2 * j + 1):
            put(m2, n, [m1[c, n] + low[c] for c in range(3)])

    coarse_stage(5, X3, 4, m4, k3, g3, lowest)
    twice_begin(6, m2)

    def raise_back(j, v, rest):
        w = relaxed(v, layer(inv2, j, 6), rest, obst2[j])
        for i in (2 * j, 2 * j + 1) if j < X2 - 1 else (2 * j + 1, 2 * j):
            old = layer(fine_ref(2), i + 1)
            w0 = jnp.where(clip[i] == 1, 0.0, w[0])
            fine_store(8, i, [old[0] + w0, old[1] + w[1], old[2] + w[2]])

    twice(6, m2, m3, raise_back)
    begin(8, (2, 3))
    fine_sweep(8, 9)
    fine_sweep(9, 10)
    fine_stage(10, lambda i, v, rest: put(resid, i, rest))
    for k in USED:
        leave(k)
    for k in TWICE:
        cross_all(k, "leave")


def local(*args):
    disp, _, heat = args[:3]
    X, Y, Z = heat.shape
    X2, X3 = X // 2, X // 4
    f32 = jnp.float32

    def buffer(*shape, dtype=f32):
        return pltpu.VMEM(shape + (Y, Z), dtype)

    rows = -(-5 * X // 8) * 8
    scratch = [
        buffer(4, X + 2),
        buffer(5, 3, X + 2),
        buffer(5, 3, X2),
        buffer(EXCHANGES, 2, 3),
        buffer(EXCHANGES, 2, 3),
        pltpu.VMEM((EXCHANGES, 2, rows, Z), f32),
        pltpu.VMEM((EXCHANGES, 2, rows, Z), f32),
        pltpu.VMEM((2, 4, 8, Z), f32),
        pltpu.VMEM((2, 4, 8, Z), f32),
        buffer(2, 16),
        pltpu.VMEM((2, X2, 12, 8, Z), f32),
        buffer(3, X),
        buffer(6, X),
        buffer(X),
        buffer(X, dtype=jnp.int32),
        buffer(X, dtype=jnp.int32),
        buffer(3, X),
        buffer(6, X),
        buffer(X),
        buffer(3, X2),
        buffer(6, X2),
        buffer(6, X2),
        buffer(X2),
        buffer(3, X3),
        buffer(6, X3),
        buffer(6, X3),
        buffer(X3),
        pltpu.SemaphoreType.DMA((8,)),
        pltpu.SemaphoreType.DMA((EXCHANGES, 4)),
        pltpu.SemaphoreType.DMA((EXCHANGES, 4)),
        pltpu.SemaphoreType.DMA((2, 4)),
        pltpu.SemaphoreType.DMA((2, 4)),
    ]
    anywhere = pl.BlockSpec(memory_space=pl.ANY)
    return pl.pallas_call(
        kernel,
        out_shape=[pltpu.VMEM(disp.shape, f32)] * 2,
        in_specs=[anywhere] * 8,
        out_specs=[pl.BlockSpec(memory_space=pltpu.VMEM)] * 2,
        scratch_shapes=scratch,
        compiler_params=pltpu.CompilerParams(collective_id=0, has_side_effects=True),
        name="vcycle",
    )(*args)


def solution(mesh):
    whole = P(None, "grp", "brick", None)
    flat = P("grp", "brick", None)
    return jax.shard_map(
        local,
        mesh=mesh,
        in_specs=(whole, whole, flat, whole, whole, flat, flat, flat),
        out_specs=(whole, whole),
        check_vma=False,
    )
```

profile of v0, /device:TPU:16, one launch (start us, length us, event | category | flops | bytes accessed | tf_op | source)
XLA Modules:
  0.0 42.4 jit_solution(1266032799325093367)
XLA Ops:
  0.6 40.4 %vcycle.1 = (f32[3,4,16,256]{3,2,1,0:T(8,128)S(1)}, f32[3,4,16,256]{3,2,1,0:T(8,128)S(1)}) custom-call(f32[3,4,16,256]{3,2,1,0:T(8,128)} %disp_h.1, f32[3,4,16,256]{3,2,1,0:T(8,128)} %load_h.1, f32[4,16,256]{2,1,0:T(8,128)} %heat_h.1, f32[3,4,16,256]{3,2,1,0:T(8,128)} %diag_h.1, f32[3,4,16,256]{3,2,1,0:T(8,128)} %off_h.1, f32[4,16,256]{2,1,0:T(8,128)} %clear_h.1, ...), custom_call_target="tpu_custom_call" | custom-call | tf_op jit(solution)/shard_map/vcycle/pallas_call | solution.py:593
  41.0 0.7 %copy.12 = f32[3,4,16,256]{3,2,1,0:T(8,128)} copy(f32[3,4,16,256]{3,2,1,0:T(8,128)S(1)} %get-tuple-element.2) | data formatting | bytes 393216
  41.7 0.7 %copy.13 = f32[3,4,16,256]{3,2,1,0:T(8,128)} copy(f32[3,4,16,256]{3,2,1,0:T(8,128)S(1)} %get-tuple-element.3) | data formatting | bytes 393216
where the time goes:
time: 42.5 us; the launch traced here: 42.4 us
  Pallas kernels  40.4 us (95%)
  local copies, waits for them, and re-layouts  1.36 us (3%)
  between operations  0.64 us (2%)
    pallas_call x1, Pallas kernels, local(): pl.pallas_call(kernel, out_shape=[pltpu.VMEM(disp.shape, f32)] * 2, in_sp...  40.4 us
    unnamed x2, local copies, waits for them, and re-layouts  1.36 us

commit v1 on v0

--- a/solution.py
+++ b/solution.py
@@ -12,6 +12,7 @@
 DEPTH = {3: 3, 4: 2, 5: 1, 6: 2}
 USED = FINE + tuple(DEPTH)
 TWICE = (3, 6)
+PIECES = 2
 MESH = pl.DeviceIdType.MESH
 
 
@@ -38,12 +39,13 @@
 def kernel(
     disp_h, load_h, heat_h, diag_h, off_h, clear_h, touch_h, clip_h,
     moved, resid,
-    first, fine, middle, xs, xr, ys, yr, ds, dr, halo_x, halo_y, load, stiff, clear, touch, clip,
-    force, inv1, obst1, g2, k2, inv2, obst2, g3, k3, inv3, obst3,
+    first, heat, fine, edge, middle, xs, xr, ys, yr, ds, dr, halo_x, halo_y, load, stiff, clear, touch, clip,
+    force, rests, inv1, obst1, g2, k2, inv2, obst2, g3, k3, inv3, obst3,
     in_sem, send_sem, recv_sem, dsend_sem, drecv_sem,
 ):
     X, Y, Z = heat_h.shape
     X2, X3 = X // 2, X // 4
+    H = Y // PIECES
     g, b = lax.axis_index("grp"), lax.axis_index("brick")
     ng, nb = lax.axis_size("grp"), lax.axis_size("brick")
     ways = (
@@ -71,8 +73,8 @@
             )
 
     pairs = (
-        (disp_h, first.at[0:3, 1 : X + 1]),
-        (heat_h, first.at[3, 1 : X + 1]),
+        (disp_h, first.at[:, 1 : X + 1]),
+        (heat_h, heat),
         (diag_h, stiff.at[0:3]),
         (off_h, stiff.at[3:6]),
         (load_h, load),
@@ -101,7 +103,7 @@
                 if way >= 2:
                     yr[k, way - 2] = jnp.zeros(yr.shape[2:], jnp.float32)
                 elif k in FINE:
-                    for c in range(4 if k == 0 else 3):
+                    for c in range(3):
                         fine_ref(k)[c, 0 if way == 0 else X + 1] = jnp.zeros((Y, Z), jnp.float32)
                 else:
                     for n in range(DEPTH[k]):
@@ -118,45 +120,47 @@
         count = 4 * X if k == 0 else 3 * X if k in FINE else {3: 10, 4: 6, 5: 3, 6: 6}[k] * X2
         return -(-count // 8) * 8
 
-    def transfer(k, way):
+    def transfer(k, way, p=0):
         if way >= 2:
             n = way - 2
             src, dst = ys.at[k, n, 0 : rows_of(k)], yr.at[k, 1 - n, 0 : rows_of(k)]
         elif k in FINE:
-            ref = fine_ref(k)
-            src, dst = ref.at[:, X if way else 1], ref.at[:, 0 if way else X + 1]
+            part = pl.ds(p * H, H)
+            src = edge.at[FINE.index(k), way, :, part]
+            dst = fine_ref(k).at[:, 0 if way else X + 1, part]
         else:
             src, dst = xs.at[k, way, 0 : DEPTH[k]], xr.at[k, 1 - way, 0 : DEPTH[k]]
         axis, there, _ = ways[way]
         return pltpu.make_async_remote_copy(
             src_ref=src,
             dst_ref=dst,
-            send_sem=send_sem.at[k, way],
-            recv_sem=recv_sem.at[k, way ^ 1],
+            send_sem=send_sem.at[k, way, p],
+            recv_sem=recv_sem.at[k, way ^ 1, p],
             device_id={axis: there},
             device_id_type=MESH,
         )
 
-    def begin(k, sides=(0, 1, 2, 3)):
+    def begin(k, sides=(0, 1, 2, 3), p=0):
         for way in sides:
 
             @pl.when(ways[way][2])
             def _():
-                transfer(k, way).start()
-
-    def arrive(k, sides):
+                transfer(k, way, p).start()
+
+    def arrive(k, sides, p=0):
         for side in sides:
 
             @pl.when(ways[side][2])
             def _():
-                transfer(k, side ^ 1).wait_recv()
+                transfer(k, side ^ 1, p).wait_recv()
 
     def leave(k):
         for way in range(4):
 
             @pl.when(ways[way][2])
             def _():
-                transfer(k, way).wait_send()
+                for p in range(PIECES if k in FINE and way < 2 else 1):
+                    transfer(k, way, p).wait_send()
 
     def cross(k, n):
         at, beyond, _ = corners[n]
@@ -270,44 +274,85 @@
         w = [OMEGA * x for x in symmetric_times(inv, right)]
         return [jnp.minimum(w[0], obstacle), w[1], w[2]]
 
-    def fine_stage(k, finish, halo=None):
+    def fine_stage(k, finish):
         ref = fine_ref(k)
-        stage(
-            k,
-            X,
-            1,
-            lambda i: layer(ref, i + 1),
-            lambda i: layer(stiff, i, 6),
-            lambda i: layer(force, i),
-            halo or (lambda side: layer(ref, (X + 1) * side)),
-            finish,
-        )
-
-    def fine_store(to, i, w):
-        put(fine_ref(to), i + 1, w)
+        for i in range(X):
+            v = layer(ref, i + 1)
+            kv = symmetric_times(layer(stiff, i, 6), v)
+            for c in range(3):
+                near = jnp.where(row < 1, 0.0, pltpu.roll(v[c], 1, 0))
+                near = near + jnp.where(row >= Y - 1, 0.0, pltpu.roll(v[c], Y - 1, 0))
+                near = near + (before(v[c], 1) + after(v[c], 1))
+                r = (force[c, i] - kv[c]) + near
+                for n in (i - 1, i + 1):
+                    if 0 <= n < X:
+                        r = r + ref[c, n + 1]
+                rests[c, i] = r
+        if k > 0:
+            arrive(k, (2, 3))
+        for i in range(X):
+            for c in range(3):
+                n = c * X + i
+                rests[c, i, 0:1, :] = rests[c, i, 0:1, :] + yr[k, 0, n : n + 1, :]
+                rests[c, i, Y - 1 : Y, :] = rests[c, i, Y - 1 : Y, :] + yr[k, 1, n : n + 1, :]
+        for i in range(1, X - 1):
+            for p in range(PIECES):
+                finish(i, p, [rests[c, i, pl.ds(p * H, H)] for c in range(3)])
+        for p in range(PIECES):
+            part = pl.ds(p * H, H)
+            for side, i in ((0, 0), (1, X - 1)):
+                arrive(k, (side,), p)
+                rest = [rests[c, i, part] + ref[c, (X + 1) * side, part] for c in range(3)]
+                if X == 1 and side == 0:
+                    for c in range(3):
+                        rests[c, i, part] = rest[c]
+                else:
+                    finish(i, p, rest)
+
+    def leave_edge(k, side, p, w):
+        part = pl.ds(p * H, H)
+        h = heat[(X - 1) * side, part]
+        edge[FINE.index(k), side, 0, part] = w[0] + h if side else w[0] - h
+        for c in (1, 2):
+            edge[FINE.index(k), side, c, part] = w[c]
+        begin(k, (side,), p)
+
+    def fine_store(to, i, p, w):
+        for c in range(3):
+            fine_ref(to)[c, i + 1, pl.ds(p * H, H)] = w[c]
         for side, end in ((0, 0), (1, X - 1)):
             if i == end:
-                begin(to, (side,))
+                leave_edge(to, side, p, w)
         for c in range(3):
-            edge_rows(to, X, c, i, w[c])
-
-    def fine_sweep(k, to, halo=None):
-        def finish(i, v, rest):
-            w = relaxed(v, layer(inv1, i, 6), rest, obst1[i])
-            fine_store(to, i, w)
+            n = c * X + i
+            if p == 0:
+                ys[to, 0, n : n + 1, :] = w[c][0:1, :]
+            if p == PIECES - 1:
+                ys[to, 1, n : n + 1, :] = w[c][H - 1 : H, :]
+
+    def fine_sweep(k, to):
+        def finish(i, p, rest):
+            part = pl.ds(p * H, H)
+            v = [fine_ref(k)[c, i + 1, part] for c in range(3)]
+            w = relaxed(v, [inv1[c, i, part] for c in range(6)], rest, obst1[i, part])
+            fine_store(to, i, p, w)
             if to == 10:
-                put(moved, i, w)
-
-        fine_stage(k, finish, halo)
+                for c in range(3):
+                    moved[c, i, part] = w[c]
+
+        fine_stage(k, finish)
         begin(to, (2, 3))
 
     arriving[0].wait()
     arriving[1].wait()
     pl.semaphore_wait(barrier, sum(jnp.where(has, 1, 0) for _, _, has in ways + tuple(corners)))
-    begin(0, (0, 1))
-    for c in range(4):
-        for i in range(X):
+    for p in range(PIECES):
+        for side in (0, 1):
+            leave_edge(0, side, p, [first[c, 1 + (X - 1) * side, pl.ds(p * H, H)] for c in range(3)])
+    for i in range(X):
+        for c in range(3):
             edge_rows(0, X, c, i, first[c, i + 1])
+        edge_rows(0, X, 3, i, heat[i])
     begin(0, (2, 3))
     for copy in arriving[2:]:
         copy.wait()
@@ -316,25 +361,17 @@
         obst1[i] = jnp.where(touch[i] == 1, clear[i], FREE)
     arrive(0, (2, 3))
     for i in range(X):
-        h = first[3, i + 1]
+        h = heat[i]
         along = load[0, i]
         if i > 0:
-            along = along + first[3, i]
+            along = along + heat[i - 1]
         if i < X - 1:
-            along = along - first[3, i + 2]
+            along = along - heat[i + 1]
         force[0, i] = along
         force[1, i] = load[1, i] - (below(0, X, 3, i, h, 1) - above(0, X, 3, i, h, 1))
         force[2, i] = load[2, i] - (after(h, 1) - before(h, 1))
 
-    def first_halo(side):
-        v = layer(first, (X + 1) * side)
-        heat = first[3, (X + 1) * side]
-        heat = heat if side == 0 else -heat
-        end = (X - 1) * side
-        force[0, end] = force[0, end] + heat
-        return [v[0] + heat, v[1], v[2]]
-
-    fine_sweep(0, 1, first_halo)
+    fine_sweep(0, 1)
     for j in range(X2):
         k = [0.125 * group(stiff[c, 2 * j], stiff[c, 2 * j + 1], 1, plus) for c in range(6)]
         put(k2, j, k)
@@ -491,11 +528,14 @@
     m0, m1, m2, m3, m4 = (middle.at[n] for n in range(5))
     fine_rests = {}
 
-    def restrict(i, v, rest):
-        fine_rests[i] = [jnp.where(clip[i] == 1, 0.0, rest[0]), rest[1], rest[2]]
+    def restrict(i, p, rest):
+        fine_rests[i, p] = [jnp.where(clip[i, pl.ds(p * H, H)] == 1, 0.0, rest[0]), rest[1], rest[2]]
         j = i // 2
-        if 2 * j in fine_rests and 2 * j + 1 in fine_rests:
-            pair = fine_rests[2 * j], fine_rests[2 * j + 1]
+        if all((n, q) in fine_rests for n in (2 * j, 2 * j + 1) for q in range(PIECES)):
+            pair = [
+                [jnp.concatenate([fine_rests[n, q][c] for q in range(PIECES)], 0) for c in range(3)]
+                for n in (2 * j, 2 * j + 1)
+            ]
             right = [0.25 * group(pair[0][c], pair[1][c], 1, plus) for c in range(3)]
             put(g2, j, right)
             put(m0, j, opened(layer(inv2, j, 6), right, obst2[j]))
@@ -532,13 +572,20 @@
         for i in (2 * j, 2 * j + 1) if j < X2 - 1 else (2 * j + 1, 2 * j):
             old = layer(fine_ref(2), i + 1)
             w0 = jnp.where(clip[i] == 1, 0.0, w[0])
-            fine_store(8, i, [old[0] + w0, old[1] + w[1], old[2] + w[2]])
+            new = [old[0] + w0, old[1] + w[1], old[2] + w[2]]
+            for p in range(PIECES):
+                fine_store(8, i, p, [x[p * H : p * H + H] for x in new])
 
     twice(6, m2, m3, raise_back)
     begin(8, (2, 3))
     fine_sweep(8, 9)
     fine_sweep(9, 10)
-    fine_stage(10, lambda i, v, rest: put(resid, i, rest))
+
+    def remain(i, p, rest):
+        for c in range(3):
+            resid[c, i, pl.ds(p * H, H)] = rest[c]
+
+    fine_stage(10, remain)
     for k in USED:
         leave(k)
     for k in TWICE:
@@ -556,8 +603,10 @@
 
     rows = -(-5 * X // 8) * 8
     scratch = [
-        buffer(4, X + 2),
+        buffer(3, X + 2),
+        buffer(X),
         buffer(5, 3, X + 2),
+        buffer(len(FINE), 2, 3),
         buffer(5, 3, X2),
         buffer(EXCHANGES, 2, 3),
         buffer(EXCHANGES, 2, 3),
@@ -573,6 +622,7 @@
         buffer(X, dtype=jnp.int32),
         buffer(X, dtype=jnp.int32),
         buffer(3, X),
+        buffer(3, X),
         buffer(6, X),
         buffer(X),
         buffer(3, X2),
@@ -584,8 +634,8 @@
         buffer(6, X3),
         buffer(X3),
         pltpu.SemaphoreType.DMA((8,)),
-        pltpu.SemaphoreType.DMA((EXCHANGES, 4)),
-        pltpu.SemaphoreType.DMA((EXCHANGES, 4)),
+        pltpu.SemaphoreType.DMA((EXCHANGES, 4, PIECES)),
+        pltpu.SemaphoreType.DMA((EXCHANGES, 4, PIECES)),
         pltpu.SemaphoreType.DMA((2, 4)),
         pltpu.SemaphoreType.DMA((2, 4)),
     ]

time: 42.5 us -> 41.5 us (0.976)
  the two profiles are of different devices: /device:TPU:16 before, /device:TPU:0 now
where the time goes in v1:
time: 41.5 us; the launch traced here: 41.4 us
  Pallas kernels  39.4 us (95%)
  local copies, waits for them, and re-layouts  1.36 us (3%)
  between operations  0.64 us (2%)
    pallas_call x1, Pallas kernels, local(): pl.pallas_call(kernel, out_shape=[pltpu.VMEM(disp.shape, f32)] * 2, in_sp...  39.4 us
    unnamed x2, local copies, waits for them, and re-layouts  1.36 us

profile of v1, /device:TPU:0, one launch (start us, length us, event | category | flops | bytes accessed | tf_op | source)
XLA Modules:
  0.0 41.4 jit_solution(15111194195706576104)
XLA Ops:
  0.6 39.4 %vcycle.1 = (f32[3,4,16,256]{3,2,1,0:T(8,128)S(1)}, f32[3,4,16,256]{3,2,1,0:T(8,128)S(1)}) custom-call(f32[3,4,16,256]{3,2,1,0:T(8,128)} %disp_h.1, f32[3,4,16,256]{3,2,1,0:T(8,128)} %load_h.1, f32[4,16,256]{2,1,0:T(8,128)} %heat_h.1, f32[3,4,16,256]{3,2,1,0:T(8,128)} %diag_h.1, f32[3,4,16,256]{3,2,1,0:T(8,128)} %off_h.1, f32[4,16,256]{2,1,0:T(8,128)} %clear_h.1, ...), custom_call_target="tpu_custom_call" | custom-call | tf_op jit(solution)/shard_map/vcycle/pallas_call | solution.py:643
  40.0 0.7 %copy.12 = f32[3,4,16,256]{3,2,1,0:T(8,128)} copy(f32[3,4,16,256]{3,2,1,0:T(8,128)S(1)} %get-tuple-element.2) | data formatting | bytes 393216
  40.7 0.7 %copy.13 = f32[3,4,16,256]{3,2,1,0:T(8,128)} copy(f32[3,4,16,256]{3,2,1,0:T(8,128)S(1)} %get-tuple-element.3) | data formatting | bytes 393216

commit v2 on v1

v2 whole, which is shorter than its diff:
```python
import jax
import jax.numpy as jnp
from jax import lax
from jax.experimental import pallas as pl
from jax.experimental.pallas import tpu as pltpu
from jax.sharding import PartitionSpec as P

OMEGA = 0.6
FREE = 1000.0
FINE = (0, 1, 2, 8, 9, 10)
PIECES = 2
RING = 2
AROUND = [(1, 0), (-1, 0), (1, 1), (1, -1), (-1, 1), (-1, -1), (2, 0), (-2, 0)]
AROUND += [(0, 1), (0, -1), (2, 1), (2, -1), (-2, 1), (-2, -1)]
STRAIGHT = [n for n, (di, dj) in enumerate(AROUND) if not (di and dj)]
DIAGONAL = [n for n, (di, dj) in enumerate(AROUND) if di and dj]
NEXT = [n for n, (di, dj) in enumerate(AROUND) if abs(di) < 2]
OPPOSITE = [AROUND.index((-di, -dj)) for di, dj in AROUND]
BLOCKS, RIGHTS = 0, 1
MESH = pl.DeviceIdType.MESH


def inverse(k, keep=None):
    a, b, c, d, e, f = k
    i00 = b * c - e * e
    i11 = a * c - f * f
    i22 = a * b - d * d
    i01 = f * e - d * c
    i12 = d * f - a * e
    i02 = d * e - b * f
    scale = 1.0 / (a * i00 + d * i01 + f * i02)
    if keep is not None:
        scale = scale * keep
    return [i00 * scale, i11 * scale, i22 * scale, i01 * scale, i12 * scale, i02 * scale]


def symmetric_times(m, v):
    return [
        m[0] * v[0] + m[3] * v[1] + m[5] * v[2],
        m[3] * v[0] + m[1] * v[1] + m[4] * v[2],
        m[5] * v[0] + m[4] * v[1] + m[2] * v[2],
    ]


def kernel(
    disp_h, load_h, heat_h, diag_h, off_h, clear_h, touch_h, clip_h,
    moved, resid,
    first, heat, fine, edge, ys, yr, load, stiff, clear, touch, clip,
    force, rests, inv1, obst1,
    squeezed, kring, gring, iring, ksend, kfrom, gsend, gfrom, m0, m1, m2, m3, inv3, m4, low,
    in_sem, send_sem, recv_sem, ring_send, ring_recv, low_send, low_recv,
):
    X, Y, Z = heat_h.shape
    X2, X3 = X // 2, X // 4
    H = Y // PIECES
    h, w = Y // 2, Z // 2
    g, b = lax.axis_index("grp"), lax.axis_index("brick")
    ng, nb = lax.axis_size("grp"), lax.axis_size("brick")
    ways = (
        ("grp", g - 1, g > 0),
        ("grp", g + 1, g < ng - 1),
        ("brick", b - 1, b > 0),
        ("brick", b + 1, b < nb - 1),
    )
    barrier = pltpu.get_barrier_semaphore()
    for axis, there, has in ways:

        @pl.when(has)
        def _():
            pl.semaphore_signal(barrier, inc=1, device_id={axis: there}, device_id_type=MESH)

    def reaches(di, dj):
        has = None
        for d, at, count in ((di, g, ng), (dj, b, nb)):
            if d:
                inside = at + d >= 0 if d < 0 else at + d < count
                has = inside if has is None else has & inside
        return has

    around = [reaches(di, dj) for di, dj in AROUND]
    for (di, dj), has in zip(AROUND, around):
        if abs(di) + abs(dj) > 1:

            @pl.when(has)
            def _():
                pl.semaphore_signal(
                    barrier, inc=1, device_id={"grp": g + di, "brick": b + dj}, device_id_type=MESH
                )

    pairs = (
        (disp_h, first.at[:, 1 : X + 1]),
        (heat_h, heat),
        (diag_h, stiff.at[0:3]),
        (off_h, stiff.at[3:6]),
        (load_h, load),
        (clear_h, clear),
        (touch_h, touch),
        (clip_h, clip),
    )
    arriving = [pltpu.make_async_copy(s, d, in_sem.at[i]) for i, (s, d) in enumerate(pairs)]
    for copy in arriving:
        copy.start()

    row = lax.broadcasted_iota(jnp.int32, (Y, Z), 0)
    lane = lax.broadcasted_iota(jnp.int32, (Y, Z), 1)
    crow = lax.broadcasted_iota(jnp.int32, (h, w), 0)
    clane = lax.broadcasted_iota(jnp.int32, (h, w), 1)
    slane = lax.broadcasted_iota(jnp.int32, (Y, w), 1)
    own, mid = pl.ds(RING * X2, X2), pl.ds(h, h)

    def fine_ref(k):
        return first if k == 0 else fine.at[FINE.index(k) - 1]

    for way, (axis, there, has) in enumerate(ways):

        @pl.when(jnp.logical_not(has))
        def _():
            for k in FINE:
                if way >= 2:
                    yr[FINE.index(k), way - 2] = jnp.zeros(yr.shape[2:], jnp.float32)
                else:
                    for c in range(3):
                        fine_ref(k)[c, 0 if way == 0 else X + 1] = jnp.zeros((Y, Z), jnp.float32)

    for n, (di, dj) in enumerate(AROUND):

        @pl.when(jnp.logical_not(around[n]))
        def _():
            for ref, fill in ((kring, (1.0,) * 3 + (0.0,) * 3), (gring, (0.0,) * 3 + (FREE,))):
                for c, x in enumerate(fill):
                    if n in DIAGONAL:
                        spot = kfrom if ref is kring else gfrom
                        spot[DIAGONAL.index(n), c] = jnp.full((h, w), x, jnp.float32)
                    else:
                        for j in range(X2):
                            ref[c, (di + RING) * X2 + j, pl.ds((dj + 1) * h, h)] = jnp.full((h, w), x, jnp.float32)
            if n in NEXT:
                for c in range(3):
                    low[c, di + 1, pl.ds((dj + 1) * h, h)] = jnp.zeros((h, w), jnp.float32)

    def transfer(k, way, p=0):
        m = FINE.index(k)
        if way >= 2:
            src, dst = ys.at[m, way - 2], yr.at[m, 3 - way]
        else:
            part = pl.ds(p * H, H)
            src = edge.at[m, way, :, part]
            dst = fine_ref(k).at[:, 0 if way else X + 1, part]
        axis, there, _ = ways[way]
        return pltpu.make_async_remote_copy(
            src_ref=src,
            dst_ref=dst,
            send_sem=send_sem.at[m, way, p],
            recv_sem=recv_sem.at[m, way ^ 1, p],
            device_id={axis: there},
            device_id_type=MESH,
        )

    def begin(k, sides=(0, 1, 2, 3), p=0):
        for way in sides:

            @pl.when(ways[way][2])
            def _():
                transfer(k, way, p).start()

    def arrive(k, sides, p=0):
        for side in sides:

            @pl.when(ways[side][2])
            def _():
                transfer(k, side ^ 1, p).wait_recv()

    def leave(k):
        for way in range(4):

            @pl.when(ways[way][2])
            def _():
                for p in range(PIECES if way < 2 else 1):
                    transfer(k, way, p).wait_send()

    def ring_copy(kind, n):
        di, dj = AROUND[n]
        m = OPPOSITE[n]
        if n in DIAGONAL:
            src = (ksend, gsend)[kind].at[0 if dj < 0 else 1]
            dst = (kfrom, gfrom)[kind].at[DIAGONAL.index(m)]
        else:
            ref = (kring, gring)[kind]
            src = ref.at[:, own, mid]
            dst = ref.at[:, pl.ds((RING - di) * X2, X2), pl.ds((1 - dj) * h, h)]
        return pltpu.make_async_remote_copy(
            src_ref=src,
            dst_ref=dst,
            send_sem=ring_send.at[kind, n],
            recv_sem=ring_recv.at[kind, m],
            device_id={"grp": g + di, "brick": b + dj},
            device_id_type=MESH,
        )

    def low_copy(n):
        di, dj = AROUND[n]
        return pltpu.make_async_remote_copy(
            src_ref=low.at[:, 1, mid],
            dst_ref=low.at[:, 1 - di, pl.ds((1 - dj) * h, h)],
            send_sem=low_send.at[n],
            recv_sem=low_recv.at[OPPOSITE[n]],
            device_id={"grp": g + di, "brick": b + dj},
            device_id_type=MESH,
        )

    def ring_begin(copy, which):
        for n in which:

            @pl.when(around[n])
            def _():
                copy(n).start()

    def ring_arrive(copy, which):
        for n in which:

            @pl.when(around[n])
            def _():
                copy(OPPOSITE[n]).wait_recv()

    def ring_leave(copy, which):
        for n in which:

            @pl.when(around[n])
            def _():
                copy(n).wait_send()

    def corners_pack(ref, out, count):
        for c in range(count):
            near, far = ref[c, RING * X2, mid], ref[c, RING * X2 + X2 - 1, mid]
            out[0, c] = jnp.where(crow < h // 2, near, pltpu.roll(far, h // 2, 0))
            out[1, c] = jnp.where(crow < h // 2, pltpu.roll(near, h // 2, 0), far)

    def corners_unpack(out, ref, count):
        for d, n in enumerate(DIAGONAL):
            di, dj = AROUND[n]
            rows = pl.ds((dj + 1) * h, h)
            for c in range(count):
                x = out[d, c]
                y = pltpu.roll(x, h // 2, 0)
                ref[c, (di + RING) * X2, rows] = y if dj < 0 else x
                ref[c, (di + RING) * X2 + X2 - 1, rows] = x if dj < 0 else y

    def edge_rows(k, layers, c, i, v):
        n = c * layers + i
        m = FINE.index(k)
        ys[m, 0, n : n + 1, :] = v[0:1, :]
        ys[m, 1, n : n + 1, :] = v[Y - 1 : Y, :]

    def before(v, s):
        at = lane if v.shape[1] == Z else clane
        return jnp.where(at < s, 0.0, pltpu.roll(v, s, 1))

    def after(v, s):
        at = lane if v.shape[1] == Z else clane
        size = v.shape[1]
        return jnp.where(at >= size - s, 0.0, pltpu.roll(v, size - s, 1))

    def above(k, layers, c, i, v, s):
        n = c * layers + i
        return jnp.where(row < s, yr[FINE.index(k), 0, n : n + 1, :], pltpu.roll(v, s, 0))

    def below(k, layers, c, i, v, s):
        n = c * layers + i
        return jnp.where(row >= Y - s, yr[FINE.index(k), 1, n : n + 1, :], pltpu.roll(v, Y - s, 0))

    def shrink(slot, v, how):
        v = how(v, pltpu.roll(v, Z - 1, 1))
        spots = (2 * slane) & (w - 1)
        lo = jnp.take_along_axis(v[:, 0:w], spots, axis=1)
        hi = jnp.take_along_axis(v[:, w:Z], spots, axis=1)
        squeezed[slot] = jnp.where(slane < w // 2, lo, hi)
        return how(squeezed[slot, pl.ds(0, h, stride=2), :], squeezed[slot, pl.ds(1, h, stride=2), :])

    def grow(slot, x):
        squeezed[slot, pl.ds(0, h, stride=2), :] = x
        squeezed[slot, pl.ds(1, h, stride=2), :] = x
        v = squeezed[slot]
        spots = slane >> 1
        parts = [jnp.take_along_axis(v, spots + n * (w // 2), axis=1) for n in (0, 1)]
        return jnp.concatenate(parts, 1)

    def pair(v, axis, how):
        size = v.shape[axis]
        at = (crow, clane)[axis]
        return how(v, jnp.where((at & 1) == 0, pltpu.roll(v, size - 1, axis), pltpu.roll(v, 1, axis)))

    def group(v, w, how):
        return pair(pair(how(v, w), 1, how), 0, how)

    def plus(v, w):
        return v + w

    def layer(ref, i, count=3):
        return [ref[c, i] for c in range(count)]

    def put(ref, i, values):
        for c, v in enumerate(values):
            ref[c, i] = v

    def relaxed(v, inv, rest, obstacle):
        step = symmetric_times(inv, rest)
        w = [v[c] + OMEGA * step[c] for c in range(3)]
        return [jnp.minimum(w[0], obstacle), w[1], w[2]]

    def opened(inv, right, obstacle):
        w = [OMEGA * x for x in symmetric_times(inv, right)]
        return [jnp.minimum(w[0], obstacle), w[1], w[2]]

    def fine_stage(k, finish):
        ref, m = fine_ref(k), FINE.index(k)
        for i in range(X):
            v = layer(ref, i + 1)
            kv = symmetric_times(layer(stiff, i, 6), v)
            for c in range(3):
                near = jnp.where(row < 1, 0.0, pltpu.roll(v[c], 1, 0))
                near = near + jnp.where(row >= Y - 1, 0.0, pltpu.roll(v[c], Y - 1, 0))
                near = near + (before(v[c], 1) + after(v[c], 1))
                r = (force[c, i] - kv[c]) + near
                for n in (i - 1, i + 1):
                    if 0 <= n < X:
                        r = r + ref[c, n + 1]
                rests[c, i] = r
        if k > 0:
            arrive(k, (2, 3))
        for i in range(X):
            for c in range(3):
                n = c * X + i
                rests[c, i, 0:1, :] = rests[c, i, 0:1, :] + yr[m, 0, n : n + 1, :]
                rests[c, i, Y - 1 : Y, :] = rests[c, i, Y - 1 : Y, :] + yr[m, 1, n : n + 1, :]
        for i in range(1, X - 1):
            for p in range(PIECES):
                finish(i, p, [rests[c, i, pl.ds(p * H, H)] for c in range(3)])
        for p in range(PIECES):
            part = pl.ds(p * H, H)
            for side, i in ((0, 0), (1, X - 1)):
                arrive(k, (side,), p)
                rest = [rests[c, i, part] + ref[c, (X + 1) * side, part] for c in range(3)]
                if X == 1 and side == 0:
                    for c in range(3):
                        rests[c, i, part] = rest[c]
                else:
                    finish(i, p, rest)

    def leave_edge(k, side, p, w):
        part = pl.ds(p * H, H)
        h = heat[(X - 1) * side, part]
        edge[FINE.index(k), side, 0, part] = w[0] + h if side else w[0] - h
        for c in (1, 2):
            edge[FINE.index(k), side, c, part] = w[c]
        begin(k, (side,), p)

    def fine_store(to, i, p, w):
        for c in range(3):
            fine_ref(to)[c, i + 1, pl.ds(p * H, H)] = w[c]
        for side, end in ((0, 0), (1, X - 1)):
            if i == end:
                leave_edge(to, side, p, w)
        for c in range(3):
            n = c * X + i
            if p == 0:
                ys[FINE.index(to), 0, n : n + 1, :] = w[c][0:1, :]
            if p == PIECES - 1:
                ys[FINE.index(to), 1, n : n + 1, :] = w[c][H - 1 : H, :]

    def fine_sweep(k, to):
        def finish(i, p, rest):
            part = pl.ds(p * H, H)
            v = [fine_ref(k)[c, i + 1, part] for c in range(3)]
            w = relaxed(v, [inv1[c, i, part] for c in range(6)], rest, obst1[i, part])
            fine_store(to, i, p, w)
            if to == 10:
                for c in range(3):
                    moved[c, i, part] = w[c]

        fine_stage(k, finish)
        begin(to, (2, 3))

    arriving[0].wait()
    arriving[1].wait()
    pl.semaphore_wait(barrier, sum(jnp.where(has, 1, 0) for has in around))
    for p in range(PIECES):
        for side in (0, 1):
            leave_edge(0, side, p, [first[c, 1 + (X - 1) * side, pl.ds(p * H, H)] for c in range(3)])
    for i in range(X):
        for c in range(3):
            edge_rows(0, X, c, i, first[c, i + 1])
        edge_rows(0, X, 3, i, heat[i])
    begin(0, (2, 3))
    for copy in arriving[2:]:
        copy.wait()
    for i in range(X):
        put(inv1, i, inverse(layer(stiff, i, 6)))
        obst1[i] = jnp.where(touch[i] == 1, clear[i], FREE)
    arrive(0, (2, 3))
    for i in range(X):
        warm = heat[i]
        along = load[0, i]
        if i > 0:
            along = along + heat[i - 1]
        if i < X - 1:
            along = along - heat[i + 1]
        force[0, i] = along
        force[1, i] = load[1, i] - (below(0, X, 3, i, warm, 1) - above(0, X, 3, i, warm, 1))
        force[2, i] = load[2, i] - (after(warm, 1) - before(warm, 1))

    for j in range(X2):
        for c in range(6):
            both = stiff[c, 2 * j] + stiff[c, 2 * j + 1]
            kring[c, RING * X2 + j, mid] = 0.125 * shrink(6 * j + c, both, plus)
    blocks_copy, rights_copy = (lambda n: ring_copy(BLOCKS, n)), (lambda n: ring_copy(RIGHTS, n))
    ring_begin(blocks_copy, STRAIGHT)
    fine_sweep(0, 1)
    corners_pack(kring, ksend, 6)
    ring_begin(blocks_copy, DIAGONAL)
    fine_sweep(1, 2)

    def block(ref, i, t, count=3):
        return [ref[c, i, t * h : t * h + h, :] for c in range(count)]

    def block_put(ref, i, t, values):
        for c, x in enumerate(values):
            ref[c, i, t * h : t * h + h, :] = x

    first_own = RING * X2
    last_own = first_own + X2 - 1

    def region(straight, sideways):
        spots = [(i, 1) for i in range(first_own - straight, last_own + straight + 1)]
        for t in (0, 2):
            spots += [(i, t) for i in range(first_own - sideways, last_own + sideways + 1)]
        return spots

    def keep(di, dj):
        if (di, dj) == (0, 0):
            return None
        return jnp.where(around[AROUND.index((di, dj))], 1.0, 0.0)

    for j in range(X2):
        gaps = []
        for i in (2 * j, 2 * j + 1):
            allowed = (touch[i] == 1) & (clip[i] == 0)
            gaps.append(jnp.where(allowed, clear[i] - fine_ref(2)[0, i + 1], FREE))
        gring[3, first_own + j, mid] = shrink(j, jnp.minimum(gaps[0], gaps[1]), jnp.minimum)
    ring_arrive(blocks_copy, range(len(AROUND)))
    corners_unpack(kfrom, kring, 6)
    for i, t in region(4, 3):
        block_put(iring, i, t, inverse(block(kring, i, t, 6), keep(i // X2 - RING, t - 1)))
    thirds = [(0, 1), (1, 1), (2, 1), (1, 0), (1, 2)]
    base = first_own - 2
    k3 = None
    for n, (q, t) in enumerate(thirds):
        pairs = [block(kring, base + 2 * q + e, t, 6) for e in (0, 1)]
        k = [0.125 * group(pairs[0][c], pairs[1][c], plus) for c in range(6)]
        if (q, t) == (1, 1):
            k3 = k
        for c, x in enumerate(inverse(k, keep(q - 1, t - 1))):
            inv3[n, c] = x
    for c in range(6):
        inv3[len(thirds), c] = k3[c]

    fine_rests = {}

    def restrict(i, p, rest):
        fine_rests[i, p] = [jnp.where(clip[i, pl.ds(p * H, H)] == 1, 0.0, rest[0]), rest[1], rest[2]]
        j = i // 2
        if all((n, q) in fine_rests for n in (2 * j, 2 * j + 1) for q in range(PIECES)):
            for c in range(3):
                both = [fine_rests[2 * j, q][c] + fine_rests[2 * j + 1, q][c] for q in range(PIECES)]
                right = 0.25 * shrink(X2 + 3 * j + c, jnp.concatenate(both, 0), plus)
                gring[c, first_own + j, mid] = right

    fine_stage(2, restrict)
    ring_begin(rights_copy, [n for n in STRAIGHT if abs(AROUND[n][0]) == 1])
    corners_pack(gring, gsend, 4)
    ring_begin(rights_copy, DIAGONAL)
    ring_begin(rights_copy, [n for n in STRAIGHT if abs(AROUND[n][0]) != 1])
    ring_arrive(rights_copy, range(len(AROUND)))
    corners_unpack(gfrom, gring, 4)

    def ring_rest(m, i, t):
        v = block(m, i, t)
        kv = symmetric_times(block(kring, i, t, 6), v)
        right = block(gring, i, t)
        rest = []
        for c in range(3):
            up = m[c, i, t * h - 1 : t * h + h - 1, :] if t > 0 else pltpu.roll(v[c], 1, 0)
            down = m[c, i, t * h + 1 : t * h + h + 1, :] if t < 2 else pltpu.roll(v[c], h - 1, 0)
            near = (up + down) + (before(v[c], 1) + after(v[c], 1))
            near = near + (m[c, i - 1, t * h : t * h + h, :] + m[c, i + 1, t * h : t * h + h, :])
            rest.append((right[c] - kv[c]) + near)
        return rest

    def ring_sweep(m, i, t):
        obstacle = gring[3, i, t * h : t * h + h, :]
        return relaxed(block(m, i, t), block(iring, i, t, 6), ring_rest(m, i, t), obstacle)

    for i, t in region(4, 3):
        obstacle = gring[3, i, t * h : t * h + h, :]
        block_put(m0, i, t, opened(block(iring, i, t, 6), block(gring, i, t), obstacle))
    for i, t in region(3, 2):
        block_put(m1, i, t, ring_sweep(m0, i, t))
    g3 = obst3 = None
    for n, (q, t) in enumerate(thirds):
        spots = (base + 2 * q, base + 2 * q + 1)
        rest = [ring_rest(m1, i, t) for i in spots]
        right = [0.25 * group(rest[0][c], rest[1][c], plus) for c in range(3)]
        gaps = [gring[3, i, t * h : t * h + h, :] - m1[0, i, t * h : t * h + h, :] for i in spots]
        obstacle = group(gaps[0], gaps[1], jnp.minimum)
        if (q, t) == (1, 1):
            g3, obst3 = right, obstacle
        block_put(m4, q, t, opened([inv3[n, c] for c in range(6)], right, obstacle))
    v = block(m4, 1, 1)
    kv = symmetric_times([inv3[len(thirds), c] for c in range(6)], v)
    rest = []
    for c in range(3):
        near = m4[c, 1, h - 2 : 2 * h - 2, :] + m4[c, 1, h + 2 : 2 * h + 2, :]
        near = near + (before(v[c], 2) + after(v[c], 2)) + (m4[c, 0, h : 2 * h, :] + m4[c, 2, h : 2 * h, :])
        rest.append((g3[c] - kv[c]) + near)
    block_put(low, 1, 1, relaxed(v, [inv3[1, c] for c in range(6)], rest, obst3))
    ring_begin(low_copy, NEXT)
    ring_arrive(low_copy, NEXT)
    for i, t in region(2, 1):
        lows = block(low, (i - base) // 2, t)
        block_put(m2, i, t, [x + y for x, y in zip(block(m1, i, t), lows)])
    for i, t in region(1, 0):
        block_put(m3, i, t, ring_sweep(m2, i, t))
    for j in (0, X2 - 1) if X2 > 1 else (0,):
        lift = [grow(3 * j + c, x) for c, x in enumerate(ring_sweep(m3, first_own + j, 1))]
        for i in (2 * j, 2 * j + 1) if j < X2 - 1 else (2 * j + 1, 2 * j):
            old = layer(fine_ref(2), i + 1)
            lift0 = jnp.where(clip[i] == 1, 0.0, lift[0])
            new = [old[0] + lift0, old[1] + lift[1], old[2] + lift[2]]
            for p in range(PIECES):
                fine_store(8, i, p, [x[p * H : p * H + H] for x in new])
    begin(8, (2, 3))
    fine_sweep(8, 9)
    fine_sweep(9, 10)

    def remain(i, p, rest):
        for c in range(3):
            resid[c, i, pl.ds(p * H, H)] = rest[c]

    fine_stage(10, remain)
    for k in FINE:
        leave(k)
    ring_leave(blocks_copy, range(len(AROUND)))
    ring_leave(rights_copy, range(len(AROUND)))
    ring_leave(low_copy, NEXT)


def local(*args):
    disp, _, heat = args[:3]
    X, Y, Z = heat.shape
    X2 = X // 2
    h, w = Y // 2, Z // 2
    f32 = jnp.float32

    def buffer(*shape, dtype=f32):
        return pltpu.VMEM(shape + (Y, Z), dtype)

    def small(*shape):
        return pltpu.VMEM(shape + (w,), f32)

    rows = -(-4 * X // 8) * 8
    layers, tall, corners = (2 * RING + 1) * X2, 3 * h, len(DIAGONAL)
    scratch = [
        buffer(3, X + 2),
        buffer(X),
        buffer(5, 3, X + 2),
        buffer(len(FINE), 2, 3),
        pltpu.VMEM((len(FINE), 2, rows, Z), f32),
        pltpu.VMEM((len(FINE), 2, rows, Z), f32),
        buffer(3, X),
        buffer(6, X),
        buffer(X),
        buffer(X, dtype=jnp.int32),
        buffer(X, dtype=jnp.int32),
        buffer(3, X),
        buffer(3, X),
        buffer(6, X),
        buffer(X),
        small(6 * X2, Y),
        small(6, layers, tall),
        small(4, layers, tall),
        small(6, layers, tall),
        small(2, 6, h),
        small(corners, 6, h),
        small(2, 4, h),
        small(corners, 4, h),
        small(3, layers, tall),
        small(3, layers, tall),
        small(3, layers, tall),
        small(3, layers, tall),
        small(6, 6, h),
        small(3, 3, tall),
        small(3, 3, tall),
        pltpu.SemaphoreType.DMA((8,)),
        pltpu.SemaphoreType.DMA((len(FINE), 4, PIECES)),
        pltpu.SemaphoreType.DMA((len(FINE), 4, PIECES)),
        pltpu.SemaphoreType.DMA((2, len(AROUND))),
        pltpu.SemaphoreType.DMA((2, len(AROUND))),
        pltpu.SemaphoreType.DMA((len(AROUND),)),
        pltpu.SemaphoreType.DMA((len(AROUND),)),
    ]
    anywhere = pl.BlockSpec(memory_space=pl.ANY)
    return pl.pallas_call(
        kernel,
        out_shape=[pltpu.VMEM(disp.shape, f32)] * 2,
        in_specs=[anywhere] * 8,
        out_specs=[pl.BlockSpec(memory_space=pltpu.VMEM)] * 2,
        scratch_shapes=scratch,
        compiler_params=pltpu.CompilerParams(collective_id=0, has_side_effects=True),
        name="vcycle",
    )(*args)


def solution(mesh):
    whole = P(None, "grp", "brick", None)
    flat = P("grp", "brick", None)
    return jax.shard_map(
        local,
        mesh=mesh,
        in_specs=(whole, whole, flat, whole, whole, flat, flat, flat),
        out_specs=(whole, whole),
        check_vma=False,
    )
```

time: 41.5 us -> 40 us (0.964)
  Pallas kernels: 39.4 us -> 37.9 us
    pallas_call x1, Pallas kernels: 39.4 us -> 37.9 us  [local(): pl.pallas_call(kernel, out_shape=[pltpu.VMEM(disp.shape, f32)] * 2, in_sp...]
where the time goes in v2:
time: 40 us; the launch traced here: 39.9 us
  Pallas kernels  37.9 us (95%)
  local copies, waits for them, and re-layouts  1.36 us (3%)
  between operations  0.64 us (2%)
    pallas_call x1, Pallas kernels, local(): pl.pallas_call(kernel, out_shape=[pltpu.VMEM(disp.shape, f32)] * 2, in_sp...  37.9 us
    unnamed x2, local copies, waits for them, and re-layouts  1.36 us

profile of v2, /device:TPU:0, one launch (start us, length us, event | category | flops | bytes accessed | tf_op | source)
XLA Modules:
  0.0 39.9 jit_solution(13294641855312652783)
XLA Ops:
  0.6 37.9 %vcycle.1 = (f32[3,4,16,256]{3,2,1,0:T(8,128)S(1)}, f32[3,4,16,256]{3,2,1,0:T(8,128)S(1)}) custom-call(f32[3,4,16,256]{3,2,1,0:T(8,128)} %disp_h.1, f32[3,4,16,256]{3,2,1,0:T(8,128)} %load_h.1, f32[4,16,256]{2,1,0:T(8,128)} %heat_h.1, f32[3,4,16,256]{3,2,1,0:T(8,128)} %diag_h.1, f32[3,4,16,256]{3,2,1,0:T(8,128)} %off_h.1, f32[4,16,256]{2,1,0:T(8,128)} %clear_h.1, ...), custom_call_target="tpu_custom_call" | custom-call | tf_op jit(solution)/shard_map/vcycle/pallas_call | solution.py:611
  38.5 0.7 %copy.12 = f32[3,4,16,256]{3,2,1,0:T(8,128)} copy(f32[3,4,16,256]{3,2,1,0:T(8,128)S(1)} %get-tuple-element.2) | data formatting | bytes 393216
  39.2 0.7 %copy.13 = f32[3,4,16,256]{3,2,1,0:T(8,128)} copy(f32[3,4,16,256]{3,2,1,0:T(8,128)S(1)} %get-tuple-element.3) | data formatting | bytes 393216

commit v3 on v2

--- a/solution.py
+++ b/solution.py
@@ -14,9 +14,13 @@
 AROUND += [(0, 1), (0, -1), (2, 1), (2, -1), (-2, 1), (-2, -1)]
 STRAIGHT = [n for n, (di, dj) in enumerate(AROUND) if not (di and dj)]
 DIAGONAL = [n for n, (di, dj) in enumerate(AROUND) if di and dj]
-NEXT = [n for n, (di, dj) in enumerate(AROUND) if abs(di) < 2]
+NEXT = [n for n, (di, dj) in enumerate(AROUND) if abs(di) < 2 or dj == 0]
+SIDES = [AROUND.index((1, 0)), AROUND.index((-1, 0))]
+CLOSE = [n for n in DIAGONAL if abs(AROUND[n][0]) == 1]
+REST = [n for n in range(len(AROUND)) if n not in SIDES + CLOSE]
+SENT = (0, 1, 2, 9, 10)
 OPPOSITE = [AROUND.index((-di, -dj)) for di, dj in AROUND]
-BLOCKS, RIGHTS = 0, 1
+BLOCKS, RIGHTS, CROSS = 0, 1, 2
 MESH = pl.DeviceIdType.MESH
 
 
@@ -48,7 +52,8 @@
     first, heat, fine, edge, ys, yr, load, stiff, clear, touch, clip,
     force, rests, inv1, obst1,
     squeezed, kring, gring, iring, ksend, kfrom, gsend, gfrom, m0, m1, m2, m3, inv3, m4, low,
-    in_sem, send_sem, recv_sem, ring_send, ring_recv, low_send, low_recv,
+    free, fedge, fhalo,
+    in_sem, send_sem, recv_sem, ring_send, ring_recv, low_send, low_recv, free_send, free_recv,
 ):
     X, Y, Z = heat_h.shape
     X2, X3 = X // 2, X // 4
@@ -115,10 +120,11 @@
 
         @pl.when(jnp.logical_not(has))
         def _():
-            for k in FINE:
+            for k in SENT:
                 if way >= 2:
                     yr[FINE.index(k), way - 2] = jnp.zeros(yr.shape[2:], jnp.float32)
                 else:
+                    fhalo[way] = jnp.zeros((Y, Z), jnp.float32)
                     for c in range(3):
                         fine_ref(k)[c, 0 if way == 0 else X + 1] = jnp.zeros((Y, Z), jnp.float32)
 
@@ -136,7 +142,7 @@
                             ref[c, (di + RING) * X2 + j, pl.ds((dj + 1) * h, h)] = jnp.full((h, w), x, jnp.float32)
             if n in NEXT:
                 for c in range(3):
-                    low[c, di + 1, pl.ds((dj + 1) * h, h)] = jnp.zeros((h, w), jnp.float32)
+                    low[c, di + RING, pl.ds((dj + 1) * h, h)] = jnp.zeros((h, w), jnp.float32)
 
     def transfer(k, way, p=0):
         m = FINE.index(k)
@@ -185,9 +191,12 @@
             src = (ksend, gsend)[kind].at[0 if dj < 0 else 1]
             dst = (kfrom, gfrom)[kind].at[DIAGONAL.index(m)]
         else:
-            ref = (kring, gring)[kind]
-            src = ref.at[:, own, mid]
-            dst = ref.at[:, pl.ds((RING - di) * X2, X2), pl.ds((1 - dj) * h, h)]
+            ref = (kring, gring, kring)[kind]
+            part = pl.ds(0, ref.shape[0])
+            if ref is kring and n in SIDES:
+                part = pl.ds(3 if kind == CROSS else 0, 3)
+            src = ref.at[part, own, mid]
+            dst = ref.at[part, pl.ds((RING - di) * X2, X2), pl.ds((1 - dj) * h, h)]
         return pltpu.make_async_remote_copy(
             src_ref=src,
             dst_ref=dst,
@@ -200,11 +209,22 @@
     def low_copy(n):
         di, dj = AROUND[n]
         return pltpu.make_async_remote_copy(
-            src_ref=low.at[:, 1, mid],
-            dst_ref=low.at[:, 1 - di, pl.ds((1 - dj) * h, h)],
+            src_ref=low.at[:, RING, mid],
+            dst_ref=low.at[:, RING - di, pl.ds((1 - dj) * h, h)],
             send_sem=low_send.at[n],
             recv_sem=low_recv.at[OPPOSITE[n]],
             device_id={"grp": g + di, "brick": b + dj},
+            device_id_type=MESH,
+        )
+
+    def free_copy(way):
+        axis, there, _ = ways[way]
+        return pltpu.make_async_remote_copy(
+            src_ref=fedge.at[way],
+            dst_ref=fhalo.at[1 - way],
+            send_sem=free_send.at[way],
+            recv_sem=free_recv.at[1 - way],
+            device_id={axis: there},
             device_id_type=MESH,
         )
 
@@ -279,7 +299,9 @@
     def grow(slot, x):
         squeezed[slot, pl.ds(0, h, stride=2), :] = x
         squeezed[slot, pl.ds(1, h, stride=2), :] = x
-        v = squeezed[slot]
+        return widen(squeezed[slot])
+
+    def widen(v):
         spots = slane >> 1
         parts = [jnp.take_along_axis(v, spots + n * (w // 2), axis=1) for n in (0, 1)]
         return jnp.concatenate(parts, 1)
@@ -325,7 +347,7 @@
                     if 0 <= n < X:
                         r = r + ref[c, n + 1]
                 rests[c, i] = r
-        if k > 0:
+        if k in SENT[1:]:
             arrive(k, (2, 3))
         for i in range(X):
             for c in range(3):
@@ -338,7 +360,8 @@
         for p in range(PIECES):
             part = pl.ds(p * H, H)
             for side, i in ((0, 0), (1, X - 1)):
-                arrive(k, (side,), p)
+                if k in SENT:
+                    arrive(k, (side,), p)
                 rest = [rests[c, i, part] + ref[c, (X + 1) * side, part] for c in range(3)]
                 if X == 1 and side == 0:
                     for c in range(3):
@@ -412,12 +435,23 @@
         for c in range(6):
             both = stiff[c, 2 * j] + stiff[c, 2 * j + 1]
             kring[c, RING * X2 + j, mid] = 0.125 * shrink(6 * j + c, both, plus)
-    blocks_copy, rights_copy = (lambda n: ring_copy(BLOCKS, n)), (lambda n: ring_copy(RIGHTS, n))
-    ring_begin(blocks_copy, STRAIGHT)
+    blocks_copy, rights_copy, cross_copy = (
+        lambda n: ring_copy(BLOCKS, n),
+        lambda n: ring_copy(RIGHTS, n),
+        lambda n: ring_copy(CROSS, n),
+    )
+    corners_pack(kring, ksend, 6)
+    ring_begin(blocks_copy, SIDES + REST)
+    for i in range(X):
+        free[i] = jnp.where(clip[i] == 1, 0.0, 1.0)
+        ys[FINE.index(1), 0, 3 * X + i : 3 * X + i + 1, :] = free[i, 0:1, :]
+        ys[FINE.index(1), 1, 3 * X + i : 3 * X + i + 1, :] = free[i, Y - 1 : Y, :]
+    for side in (0, 1):
+        fedge[side] = free[(X - 1) * side]
     fine_sweep(0, 1)
-    corners_pack(kring, ksend, 6)
-    ring_begin(blocks_copy, DIAGONAL)
+    ring_begin(cross_copy, SIDES)
     fine_sweep(1, 2)
+    ring_begin(blocks_copy, CLOSE)
 
     def block(ref, i, t, count=3):
         return [ref[c, i, t * h : t * h + h, :] for c in range(count)]
@@ -446,7 +480,30 @@
             allowed = (touch[i] == 1) & (clip[i] == 0)
             gaps.append(jnp.where(allowed, clear[i] - fine_ref(2)[0, i + 1], FREE))
         gring[3, first_own + j, mid] = shrink(j, jnp.minimum(gaps[0], gaps[1]), jnp.minimum)
+    fine_rests = {}
+
+    def restrict(i, p, rest):
+        fine_rests[i, p] = [jnp.where(clip[i, pl.ds(p * H, H)] == 1, 0.0, rest[0]), rest[1], rest[2]]
+        j = i // 2
+        if all((n, q) in fine_rests for n in (2 * j, 2 * j + 1) for q in range(PIECES)):
+            for c in range(3):
+                both = [fine_rests[2 * j, q][c] + fine_rests[2 * j + 1, q][c] for q in range(PIECES)]
+                right = 0.25 * shrink(X2 + 3 * j + c, jnp.concatenate(both, 0), plus)
+                gring[c, first_own + j, mid] = right
+
+    fine_stage(2, restrict)
+    ring_begin(rights_copy, [n for n in STRAIGHT if abs(AROUND[n][0]) == 1])
+    corners_pack(gring, gsend, 4)
+    ring_begin(rights_copy, DIAGONAL)
+    ring_begin(rights_copy, [n for n in STRAIGHT if abs(AROUND[n][0]) != 1])
+    for way in (0, 1):
+
+        @pl.when(ways[way][2])
+        def _():
+            free_copy(way).start()
+
     ring_arrive(blocks_copy, range(len(AROUND)))
+    ring_arrive(cross_copy, SIDES)
     corners_unpack(kfrom, kring, 6)
     for i, t in region(4, 3):
         block_put(iring, i, t, inverse(block(kring, i, t, 6), keep(i // X2 - RING, t - 1)))
@@ -463,22 +520,6 @@
     for c in range(6):
         inv3[len(thirds), c] = k3[c]
 
-    fine_rests = {}
-
-    def restrict(i, p, rest):
-        fine_rests[i, p] = [jnp.where(clip[i, pl.ds(p * H, H)] == 1, 0.0, rest[0]), rest[1], rest[2]]
-        j = i // 2
-        if all((n, q) in fine_rests for n in (2 * j, 2 * j + 1) for q in range(PIECES)):
-            for c in range(3):
-                both = [fine_rests[2 * j, q][c] + fine_rests[2 * j + 1, q][c] for q in range(PIECES)]
-                right = 0.25 * shrink(X2 + 3 * j + c, jnp.concatenate(both, 0), plus)
-                gring[c, first_own + j, mid] = right
-
-    fine_stage(2, restrict)
-    ring_begin(rights_copy, [n for n in STRAIGHT if abs(AROUND[n][0]) == 1])
-    corners_pack(gring, gsend, 4)
-    ring_begin(rights_copy, DIAGONAL)
-    ring_begin(rights_copy, [n for n in STRAIGHT if abs(AROUND[n][0]) != 1])
     ring_arrive(rights_copy, range(len(AROUND)))
     corners_unpack(gfrom, gring, 4)
 
@@ -521,23 +562,48 @@
         near = m4[c, 1, h - 2 : 2 * h - 2, :] + m4[c, 1, h + 2 : 2 * h + 2, :]
         near = near + (before(v[c], 2) + after(v[c], 2)) + (m4[c, 0, h : 2 * h, :] + m4[c, 2, h : 2 * h, :])
         rest.append((g3[c] - kv[c]) + near)
-    block_put(low, 1, 1, relaxed(v, [inv3[1, c] for c in range(6)], rest, obst3))
+    block_put(low, RING, 1, relaxed(v, [inv3[1, c] for c in range(6)], rest, obst3))
     ring_begin(low_copy, NEXT)
     ring_arrive(low_copy, NEXT)
+    for i, t in region(3, 2):
+        lows = block(low, i // X2, t)
+        block_put(m2, i, t, [x + y for x, y in zip(block(m1, i, t), lows)])
     for i, t in region(2, 1):
-        lows = block(low, (i - base) // 2, t)
-        block_put(m2, i, t, [x + y for x, y in zip(block(m1, i, t), lows)])
+        block_put(m3, i, t, ring_sweep(m2, i, t))
     for i, t in region(1, 0):
-        block_put(m3, i, t, ring_sweep(m2, i, t))
-    for j in (0, X2 - 1) if X2 > 1 else (0,):
-        lift = [grow(3 * j + c, x) for c, x in enumerate(ring_sweep(m3, first_own + j, 1))]
-        for i in (2 * j, 2 * j + 1) if j < X2 - 1 else (2 * j + 1, 2 * j):
+        block_put(m0, i, t, ring_sweep(m3, i, t))
+    for j in range(X2):
+        lift = [grow(3 * j + c, x) for c, x in enumerate(block(m0, first_own + j, 1))]
+        for i in (2 * j, 2 * j + 1):
             old = layer(fine_ref(2), i + 1)
-            lift0 = jnp.where(clip[i] == 1, 0.0, lift[0])
-            new = [old[0] + lift0, old[1] + lift[1], old[2] + lift[2]]
-            for p in range(PIECES):
-                fine_store(8, i, p, [x[p * H : p * H + H] for x in new])
-    begin(8, (2, 3))
+            put(fine_ref(8), i + 1, [old[0] + free[i] * lift[0], old[1] + lift[1], old[2] + lift[2]])
+    for way in (0, 1):
+
+        @pl.when(ways[way][2])
+        def _():
+            free_copy(way ^ 1).wait_recv()
+
+    for side, i in ((0, first_own - 1), (1, last_own + 1)):
+        lift = [grow(3 * (X2 + side) + c, x) for c, x in enumerate(block(m0, i, 1))]
+        old = layer(fine_ref(2), (X + 1) * side)
+        put(fine_ref(8), (X + 1) * side, [old[0] + fhalo[side] * lift[0], old[1] + lift[1], old[2] + lift[2]])
+    spots = [(side, c, j) for side in (0, 1) for c in range(3) for j in range(X2)]
+    top = 3 * (X2 + 2)
+    for n, (side, c, j) in enumerate(spots):
+        at = 2 * h if side else h - 1
+        squeezed[top + n // Y, n % Y : n % Y + 1, :] = m0[c, first_own + j, at : at + 1, :]
+    last = FINE.index(2)
+    for n, (side, c, j) in enumerate(spots):
+        if n % Y == 0:
+            lift = widen(squeezed[top + n // Y])
+        line = lift[n % Y : n % Y + 1, :]
+        for i in (2 * j, 2 * j + 1):
+            x = line
+            if c == 0:
+                x = line * yr[FINE.index(1), side, 3 * X + i : 3 * X + i + 1, :]
+            yr[FINE.index(8), side, c * X + i : c * X + i + 1, :] = (
+                yr[last, side, c * X + i : c * X + i + 1, :] + x
+            )
     fine_sweep(8, 9)
     fine_sweep(9, 10)
 
@@ -546,8 +612,15 @@
             resid[c, i, pl.ds(p * H, H)] = rest[c]
 
     fine_stage(10, remain)
-    for k in FINE:
+    for k in SENT:
         leave(k)
+    for way in (0, 1):
+
+        @pl.when(ways[way][2])
+        def _():
+            free_copy(way).wait_send()
+
+    ring_leave(cross_copy, SIDES)
     ring_leave(blocks_copy, range(len(AROUND)))
     ring_leave(rights_copy, range(len(AROUND)))
     ring_leave(low_copy, NEXT)
@@ -584,7 +657,7 @@
         buffer(3, X),
         buffer(6, X),
         buffer(X),
-        small(6 * X2, Y),
+        small(3 * (X2 + 2) - (-6 * X2 // Y), Y),
         small(6, layers, tall),
         small(4, layers, tall),
         small(6, layers, tall),
@@ -598,14 +671,19 @@
         small(3, layers, tall),
         small(6, 6, h),
         small(3, 3, tall),
-        small(3, 3, tall),
+        small(3, 2 * RING + 1, tall),
+        buffer(X),
+        buffer(2),
+        buffer(2),
         pltpu.SemaphoreType.DMA((8,)),
         pltpu.SemaphoreType.DMA((len(FINE), 4, PIECES)),
         pltpu.SemaphoreType.DMA((len(FINE), 4, PIECES)),
-        pltpu.SemaphoreType.DMA((2, len(AROUND))),
-        pltpu.SemaphoreType.DMA((2, len(AROUND))),
+        pltpu.SemaphoreType.DMA((3, len(AROUND))),
+        pltpu.SemaphoreType.DMA((3, len(AROUND))),
         pltpu.SemaphoreType.DMA((len(AROUND),)),
         pltpu.SemaphoreType.DMA((len(AROUND),)),
+        pltpu.SemaphoreType.DMA((2,)),
+        pltpu.SemaphoreType.DMA((2,)),
     ]
     anywhere = pl.BlockSpec(memory_space=pl.ANY)
     return pl.pallas_call(

time: 40 us -> 37.1 us (0.927)
  Pallas kernels: 37.9 us -> 35 us
    pallas_call x1, Pallas kernels: 37.9 us -> 35 us  [local(): pl.pallas_call(kernel, out_shape=[pltpu.VMEM(disp.shape, f32)] * 2, in_sp...]
where the time goes in v3:
time: 37.1 us; the launch traced here: 37 us
  Pallas kernels  35 us (94%)
  local copies, waits for them, and re-layouts  1.36 us (4%)
  between operations  0.64 us (2%)
    pallas_call x1, Pallas kernels, local(): pl.pallas_call(kernel, out_shape=[pltpu.VMEM(disp.shape, f32)] * 2, in_sp...  35 us
    unnamed x2, local copies, waits for them, and re-layouts  1.36 us

profile of v3, /device:TPU:0, one launch (start us, length us, event | category | flops | bytes accessed | tf_op | source)
XLA Modules:
  0.0 37.0 jit_solution(6380542084034146265)
XLA Ops:
  0.6 35.0 %vcycle.1 = (f32[3,4,16,256]{3,2,1,0:T(8,128)S(1)}, f32[3,4,16,256]{3,2,1,0:T(8,128)S(1)}) custom-call(f32[3,4,16,256]{3,2,1,0:T(8,128)} %disp_h.1, f32[3,4,16,256]{3,2,1,0:T(8,128)} %load_h.1, f32[4,16,256]{2,1,0:T(8,128)} %heat_h.1, f32[3,4,16,256]{3,2,1,0:T(8,128)} %diag_h.1, f32[3,4,16,256]{3,2,1,0:T(8,128)} %off_h.1, f32[4,16,256]{2,1,0:T(8,128)} %clear_h.1, ...), custom_call_target="tpu_custom_call" | custom-call | tf_op jit(solution)/shard_map/vcycle/pallas_call | solution.py:689
  35.6 0.7 %copy.12 = f32[3,4,16,256]{3,2,1,0:T(8,128)} copy(f32[3,4,16,256]{3,2,1,0:T(8,128)S(1)} %get-tuple-element.2) | data formatting | bytes 393216
  36.3 0.7 %copy.13 = f32[3,4,16,256]{3,2,1,0:T(8,128)} copy(f32[3,4,16,256]{3,2,1,0:T(8,128)S(1)} %get-tuple-element.3) | data formatting | bytes 393216

commit v4 on v3

--- a/solution.py
+++ b/solution.py
@@ -335,7 +335,7 @@
 
     def fine_stage(k, finish):
         ref, m = fine_ref(k), FINE.index(k)
-        for i in range(X):
+        for i in sorted(range(X), key=lambda i: i not in (0, X - 1)):
             v = layer(ref, i + 1)
             kv = symmetric_times(layer(stiff, i, 6), v)
             for c in range(3):
@@ -354,9 +354,16 @@
                 n = c * X + i
                 rests[c, i, 0:1, :] = rests[c, i, 0:1, :] + yr[m, 0, n : n + 1, :]
                 rests[c, i, Y - 1 : Y, :] = rests[c, i, Y - 1 : Y, :] + yr[m, 1, n : n + 1, :]
-        for i in range(1, X - 1):
-            for p in range(PIECES):
-                finish(i, p, [rests[c, i, pl.ds(p * H, H)] for c in range(3)])
+
+        def inside():
+            for i in range(1, X - 1):
+                for p in range(PIECES):
+                    finish(i, p, [rests[c, i, pl.ds(p * H, H)] for c in range(3)])
+
+        if k in SENT:
+            inside()
+        if k == SENT[-1]:
+            leave_all()
         for p in range(PIECES):
             part = pl.ds(p * H, H)
             for side, i in ((0, 0), (1, X - 1)):
@@ -368,6 +375,8 @@
                         rests[c, i, part] = rest[c]
                 else:
                     finish(i, p, rest)
+        if k not in SENT:
+            inside()
 
     def leave_edge(k, side, p, w):
         part = pl.ds(p * H, H)
@@ -611,19 +620,22 @@
         for c in range(3):
             resid[c, i, pl.ds(p * H, H)] = rest[c]
 
+    def leave_all():
+        for k in SENT[:-1]:
+            leave(k)
+        for way in (0, 1):
+
+            @pl.when(ways[way][2])
+            def _():
+                free_copy(way).wait_send()
+
+        ring_leave(cross_copy, SIDES)
+        ring_leave(blocks_copy, range(len(AROUND)))
+        ring_leave(rights_copy, range(len(AROUND)))
+        ring_leave(low_copy, NEXT)
+
     fine_stage(10, remain)
-    for k in SENT:
-        leave(k)
-    for way in (0, 1):
-
-        @pl.when(ways[way][2])
-        def _():
-            free_copy(way).wait_send()
-
-    ring_leave(cross_copy, SIDES)
-    ring_leave(blocks_copy, range(len(AROUND)))
-    ring_leave(rights_copy, range(len(AROUND)))
-    ring_leave(low_copy, NEXT)
+    leave(SENT[-1])
 
 
 def local(*args):

time: 37.1 us -> 37 us (level)
  no operation moved by 1% of the time
where the time goes in v4:
time: 37 us; the launch traced here: 36.9 us
  Pallas kernels  34.9 us (94%)
  local copies, waits for them, and re-layouts  1.36 us (4%)
  between operations  0.64 us (2%)
    pallas_call x1, Pallas kernels, local(): pl.pallas_call(kernel, out_shape=[pltpu.VMEM(disp.shape, f32)] * 2, in_sp...  34.9 us
    unnamed x2, local copies, waits for them, and re-layouts  1.36 us

profile of v4, /device:TPU:0, one launch (start us, length us, event | category | flops | bytes accessed | tf_op | source)
XLA Modules:
  0.0 36.9 jit_solution(1974152529287789422)
XLA Ops:
  0.6 34.9 %vcycle.1 = (f32[3,4,16,256]{3,2,1,0:T(8,128)S(1)}, f32[3,4,16,256]{3,2,1,0:T(8,128)S(1)}) custom-call(f32[3,4,16,256]{3,2,1,0:T(8,128)} %disp_h.1, f32[3,4,16,256]{3,2,1,0:T(8,128)} %load_h.1, f32[4,16,256]{2,1,0:T(8,128)} %heat_h.1, f32[3,4,16,256]{3,2,1,0:T(8,128)} %diag_h.1, f32[3,4,16,256]{3,2,1,0:T(8,128)} %off_h.1, f32[4,16,256]{2,1,0:T(8,128)} %clear_h.1, ...), custom_call_target="tpu_custom_call" | custom-call | tf_op jit(solution)/shard_map/vcycle/pallas_call | solution.py:701
  35.5 0.7 %copy.12 = f32[3,4,16,256]{3,2,1,0:T(8,128)} copy(f32[3,4,16,256]{3,2,1,0:T(8,128)S(1)} %get-tuple-element.2) | data formatting | bytes 393216
  36.2 0.7 %copy.13 = f32[3,4,16,256]{3,2,1,0:T(8,128)} copy(f32[3,4,16,256]{3,2,1,0:T(8,128)S(1)} %get-tuple-element.3) | data formatting | bytes 393216

commit v5 on v4

--- a/solution.py
+++ b/solution.py
@@ -636,6 +636,17 @@
 
     fine_stage(10, remain)
     leave(SENT[-1])
+
+
+def flush(moved, resid, moved_h, resid_h, sem):
+    copies = [
+        pltpu.make_async_copy(moved, moved_h, sem.at[0]),
+        pltpu.make_async_copy(resid, resid_h, sem.at[1]),
+    ]
+    for copy in copies:
+        copy.start()
+    for copy in copies:
+        copy.wait()
 
 
 def local(*args):
@@ -698,7 +709,7 @@
         pltpu.SemaphoreType.DMA((2,)),
     ]
     anywhere = pl.BlockSpec(memory_space=pl.ANY)
-    return pl.pallas_call(
+    outs = pl.pallas_call(
         kernel,
         out_shape=[pltpu.VMEM(disp.shape, f32)] * 2,
         in_specs=[anywhere] * 8,
@@ -707,6 +718,14 @@
         compiler_params=pltpu.CompilerParams(collective_id=0, has_side_effects=True),
         name="vcycle",
     )(*args)
+    return pl.pallas_call(
+        flush,
+        out_shape=[jax.ShapeDtypeStruct(disp.shape, f32)] * 2,
+        in_specs=[pl.BlockSpec(memory_space=pltpu.VMEM)] * 2,
+        out_specs=[anywhere] * 2,
+        scratch_shapes=[pltpu.SemaphoreType.DMA((2,))],
+        name="flush",
+    )(*[pltpu.with_memory_space_constraint(x, pltpu.VMEM) for x in outs])
 
 
 def solution(mesh):

time: 37 us -> 36.4 us (0.984)
  local copies, waits for them, and re-layouts: 1.36 us -> 0 us
  Pallas kernels: 34.9 us -> 35.6 us
    unnamed x2 -> x0, local copies, waits for them, and re-layouts: 1.36 us -> none
    pallas_call x0 -> x1, Pallas kernels: none -> 0.76 us  [local(): pl.pallas_call(flush, out_shape=[jax.ShapeDtypeStruct(disp.shape, f32)] *...]
where the time goes in v5:
time: 36.4 us; the launch traced here: 36.3 us
  Pallas kernels  35.6 us (98%)
  between operations  0.64 us (2%)
    pallas_call x1, Pallas kernels, local(): pl.pallas_call(kernel, out_shape=[pltpu.VMEM(disp.shape, f32)] * 2, in_sp...  34.9 us
    pallas_call x1, Pallas kernels, local(): pl.pallas_call(flush, out_shape=[jax.ShapeDtypeStruct(disp.shape, f32)] *...  0.76 us

profile of v5, /device:TPU:0, one launch (start us, length us, event | category | flops | bytes accessed | tf_op | source)
XLA Modules:
  0.0 36.3 jit_solution(12307177882930286199)
XLA Ops:
  0.6 34.9 %vcycle.1 = (f32[3,4,16,256]{3,2,1,0:T(8,128)S(1)}, f32[3,4,16,256]{3,2,1,0:T(8,128)S(1)}) custom-call(f32[3,4,16,256]{3,2,1,0:T(8,128)} %disp_h.1, f32[3,4,16,256]{3,2,1,0:T(8,128)} %load_h.1, f32[4,16,256]{2,1,0:T(8,128)} %heat_h.1, f32[3,4,16,256]{3,2,1,0:T(8,128)} %diag_h.1, f32[3,4,16,256]{3,2,1,0:T(8,128)} %off_h.1, f32[4,16,256]{2,1,0:T(8,128)} %clear_h.1, ...), custom_call_target="tpu_custom_call" | custom-call | tf_op jit(solution)/shard_map/vcycle/pallas_call | solution.py:712
  35.5 0.8 %flush.1 = (f32[3,4,16,256]{3,2,1,0:T(8,128)}, f32[3,4,16,256]{3,2,1,0:T(8,128)}) custom-call(f32[3,4,16,256]{3,2,1,0:T(8,128)S(1)} %get-tuple-element.4.moved, f32[3,4,16,256]{3,2,1,0:T(8,128)S(1)} %get-tuple-element.5.resid), custom_call_target="tpu_custom_call" | custom-call | tf_op jit(solution)/shard_map/flush/pallas_call | solution.py:721
